TPU v7x, 32 devices: a whole 2x2x4 slice. The times are simulated.
32 devices in a mesh: data: 2 (over x), cp: 4 (over z), tp: 4 (over y, core).
Axes of the slice: x: 2, y: 2, z: 4, core: 2. Of those that a mesh axis runs over, the one named last changes fastest.
Arguments:
- act_in: bfloat16 [2, 6144, 3584], P(None, ('data', 'cp', 'tp')), parts along dimension 1
- route_ids: int32 [2, 6144, 2], P(None, ('data', 'cp', 'tp')), parts along dimension 1
- route_gates: float32 [2, 6144, 2], P(None, ('data', 'cp', 'tp')), parts along dimension 1
- w_query: bfloat16 [3584, 28, 128], P(None, 'tp')
- w_key: bfloat16 [3584, 4, 128], P(None, 'tp')
- w_value: bfloat16 [3584, 4, 128], P(None, 'tp')
- w_out: bfloat16 [28, 128, 3584], P('tp')
- w_gate: bfloat16 [16, 3584, 2560], P(('cp', 'tp'))
- w_up: bfloat16 [16, 3584, 2560], P(('cp', 'tp'))
- w_down: bfloat16 [16, 2560, 3584], P(('cp', 'tp'))
Outputs:
- output: bfloat16 [2, 6144, 3584], P(None, ('data', 'cp', 'tp')), parts along dimension 1
There are 2 independent parts. A program takes and returns all parts, laid end to end along the dimension named above; an argument that names none is the same for every part.
All inputs are finite; a program needn't handle non-finite values.
Results may differ from a plain program's by a relative error of at most 0.00542754.
Values are sent between devices in bfloat16 or wider.
A program may use at most 1 GiB of HBM per device.

v0:
```python
import jax
import jax.numpy as jnp
from jax import lax
from jax.sharding import PartitionSpec as P


def pick_rows(row_table, row_ids):
    return jnp.take(row_table, row_ids, axis=0, mode='fill', fill_value=0)


def attend_local(act_in, w_query, w_key, w_value, w_out, cp_size, tp_size):
    n_micro, tokens, hidden = act_in.shape
    q_local, head_dim = w_query.shape[1], w_query.shape[2]
    kv_local = w_key.shape[1]
    group_size = q_local // kv_local
    half_rows = tokens * tp_size
    piece_len = half_rows // 2
    seq_len = half_rows * cp_size
    cp_rank = lax.axis_index('cp')
    x_half = lax.all_gather(act_in, 'tp', axis=1, tiled=True)
    query_rows = jnp.einsum('bsh,hnd->bsnd', x_half, w_query, preferred_element_type=jnp.float32).astype(jnp.bfloat16)
    query_rows = query_rows.reshape(n_micro, half_rows, kv_local, group_size, head_dim)
    key_half = jnp.einsum('bsh,hnd->bsnd', x_half, w_key, preferred_element_type=jnp.float32).astype(jnp.bfloat16)
    value_half = jnp.einsum('bsh,hnd->bsnd', x_half, w_value, preferred_element_type=jnp.float32).astype(jnp.bfloat16)
    key_all = lax.all_gather(key_half, 'cp', axis=1, tiled=True)
    value_all = lax.all_gather(value_half, 'cp', axis=1, tiled=True)
    local_ix = jnp.arange(half_rows)
    owner_ix = jnp.arange(cp_size)[:, None]
    key_pos = jnp.where(local_ix < piece_len, owner_ix * piece_len + local_ix, (2 * cp_size - 1 - owner_ix) * piece_len + local_ix - piece_len).reshape(seq_len)
    score_scale = head_dim ** -0.5
    halves = []
    for half_id in range(2):
        piece_id = cp_rank if half_id == 0 else 2 * cp_size - 1 - cp_rank
        query_pos = piece_id * piece_len + jnp.arange(piece_len)
        q_part = query_rows[:, half_id * piece_len:(half_id + 1) * piece_len]
        scores = jnp.einsum('bqhgd,bkhd->bhgqk', q_part, key_all, preferred_element_type=jnp.float32) * score_scale
        scores = jnp.where(key_pos[None, :] <= query_pos[:, None], scores, -jnp.inf)
        row_peak = jnp.max(scores, axis=-1, keepdims=True)
        exp_scores = jnp.exp(scores - row_peak)
        row_sum = jnp.sum(exp_scores, axis=-1)
        weighted = jnp.einsum('bhgqk,bkhd->bqhgd', exp_scores.astype(jnp.bfloat16), value_all, preferred_element_type=jnp.float32)
        weighted = weighted / jnp.transpose(row_sum, (0, 3, 1, 2))[..., None]
        halves.append(weighted.astype(jnp.bfloat16))
    attn_rows = jnp.concatenate(halves, axis=1).reshape(n_micro, half_rows, q_local, head_dim)
    partial = jnp.einsum('bsnd,ndh->bsh', attn_rows, w_out, preferred_element_type=jnp.float32)
    attn_sum = lax.psum_scatter(partial, 'tp', scatter_dimension=1, tiled=True)
    return (act_in.astype(jnp.float32) + attn_sum).astype(jnp.bfloat16)


def dispatch_experts(mid_rows, route_ids, route_gates, w_gate, w_up, w_down, experts):
    n_micro, tokens, hidden = mid_rows.shape
    capacity = (4 * tokens) // experts
    flat_ids = route_ids.reshape(n_micro, 2 * tokens)
    expert_hits = (flat_ids[..., None] == jnp.arange(experts)).astype(jnp.int32)
    slot_rank = jnp.sum((jnp.cumsum(expert_hits, axis=1) - 1) * expert_hits, axis=-1)
    dest_slot = flat_ids * capacity + slot_rank
    micro_ix = jnp.arange(n_micro)[:, None]
    token_of = jnp.broadcast_to((jnp.arange(2 * tokens, dtype=jnp.int32) // 2)[None, :], dest_slot.shape)
    source_row = jnp.full((n_micro, experts * capacity), tokens, jnp.int32).at[micro_ix, dest_slot].set(token_of)
    send_buf = jax.vmap(pick_rows)(mid_rows, source_row).reshape(n_micro, experts, capacity, hidden)
    recv_buf = lax.all_to_all(send_buf, ('cp', 'tp'), 1, 1, tiled=True)
    expert_in = recv_buf.reshape(n_micro, experts * capacity, hidden)
    gate_act = jnp.einsum('bth,hf->btf', expert_in, w_gate[0], preferred_element_type=jnp.float32)
    up_act = jnp.einsum('bth,hf->btf', expert_in, w_up[0], preferred_element_type=jnp.float32)
    mixed_act = (jax.nn.silu(gate_act) * up_act).astype(jnp.bfloat16)
    expert_out = jnp.einsum('btf,fh->bth', mixed_act, w_down[0], preferred_element_type=jnp.float32).astype(jnp.bfloat16)
    back_buf = lax.all_to_all(expert_out.reshape(n_micro, experts, capacity, hidden), ('cp', 'tp'), 1, 1, tiled=True)
    picked = jax.vmap(pick_rows)(back_buf.reshape(n_micro, experts * capacity, hidden), dest_slot).reshape(n_micro, tokens, 2, hidden)
    combined = route_gates[:, :, 0:1] * picked[:, :, 0].astype(jnp.float32) + route_gates[:, :, 1:2] * picked[:, :, 1].astype(jnp.float32)
    return (mid_rows.astype(jnp.float32) + combined).astype(jnp.bfloat16)


def solution(mesh):
    cp_size = mesh.shape['cp']
    tp_size = mesh.shape['tp']
    experts = cp_size * tp_size
    row_spec = P(None, ('data', 'cp', 'tp'), None)
    head_spec = P(None, 'tp', None)
    out_spec = P('tp', None, None)
    expert_spec = P(('cp', 'tp'), None, None)

    def device_step(act_in, route_ids, route_gates, w_query, w_key, w_value, w_out, w_gate, w_up, w_down):
        mid_rows = attend_local(act_in, w_query, w_key, w_value, w_out, cp_size, tp_size)
        return dispatch_experts(mid_rows, route_ids, route_gates, w_gate, w_up, w_down, experts)

    return jax.shard_map(device_step, mesh=mesh, in_specs=(row_spec, row_spec, row_spec, head_spec, head_spec, head_spec, out_spec, expert_spec, expert_spec, expert_spec), out_specs=row_spec, check_vma=False)
```

profile of v0, /device:TPU:13, one launch (start us, length us, event | category | flops | bytes accessed | tf_op | source)
XLA Modules:
  0.0 1155.1 jit_solution(16855403477389375791)
XLA Ops:
  7.3 75.9 %all-gather.6.cloned.1.call-done = bf16[2,768,3584]{2,1,0:T(8,128)(2,1)} async-done(((bf16[2,192,3584]{2,1,0:T(8,128)(2,1)}), bf16[2,768,3584]{2,1,0:T(8,128)(2,1)}) %all-gather.6.cloned.1.call-update) | async-done | bytes 11010064 | tf_op jit(solution)/shard_map/all_gather | solution.py:20
  83.2 6.6 convolution_convert_fusion
  90.0 1.6 broadcast_compare_fusion.1
  91.6 6.6 convolution_convert_fusion.1
  98.5 16.8 %convert_bitcast_fusion = bf16[2,768,1,7,128]{4,1,3,0,2:T(8,128)(2,1)} fusion(bf16[3584,7,128]{2,0,1:T(8,128)(2,1)} %param.13, bf16[2,768,3584]{2,1,0:T(8,128)(2,1)} %all-gather.6.cloned.1.call-done), kind=kOutput, calls=%fused_computation.49 | convolution fusion | flops 9866379264 | bytes 20185088 | tf_op jit(solution)/shard_map/bsh,hnd->bsnd/dot_general | solution.py:21
  115.3 10.2 all-gather.10.cloned.1.call-done
  125.5 25.4 %fusion.4 = (f32[2,7,384]{2,1,0:T(8,128)S(1)}, f32[2,3072,384,7]{2,1,3,0:T(8,128)}) fusion(pred[384,3072]{0,1:T(8,128)(4,1)S(1)} %get-tuple-element.5, bf16[2,768,1,7,128]{4,1,3,0,2:T(8,128)(2,1)} %convert_bitcast_fusion, bf16[2,3072,128]{2,1,0:T(8,128)(2,1)} %all-gather.10.cloned.1.call-done), kind=kOutput, calls=%fused_computation.11 | convolution fusion | flops 4277398272 | bytes 70210560 | tf_op jit(solution)/shard_map/bqhgd,bkhd->bhgqk/dot_general | solution.py:36
  150.9 21.0 %fusion = f32[2,7,384]{2,1,0:T(8,128)S(1)} fusion(f32[2,3072,384,7]{2,1,3,0:T(8,128)} %get-tuple-element.14, f32[2,7,384]{2,1,0:T(8,128)S(1)} %get-tuple-element.13, pred[384,3072]{0,1:T(8,128)(4,1)S(1)} %get-tuple-element.5), kind=kLoop, calls=%fused_computation.7 | loop fusion | flops 66054912 | bytes 67282944 | tf_op jit(solution)/shard_map/reduce_sum | solution.py:40
  171.8 25.6 %fusion.5 = (f32[2,7,384]{2,1,0:T(8,128)S(1)}, f32[2,3072,384,7]{2,1,3,0:T(8,128)}) fusion(pred[384,3072]{0,1:T(8,128)(4,1)S(1)} %get-tuple-element.6, bf16[2,768,1,7,128]{4,1,3,0,2:T(8,128)(2,1)} %convert_bitcast_fusion, bf16[2,3072,128]{2,1,0:T(8,128)(2,1)} %all-gather.10.cloned.1.call-done), kind=kOutput, calls=%fused_computation.12 | convolution fusion | flops 4277398272 | bytes 70210560 | tf_op jit(solution)/shard_map/bqhgd,bkhd->bhgqk/dot_general | solution.py:36
  197.4 21.0 %fusion.2 = f32[2,7,384]{2,1,0:T(8,128)S(1)} fusion(f32[2,3072,384,7]{2,1,3,0:T(8,128)} %get-tuple-element.12, f32[2,7,384]{2,1,0:T(8,128)S(1)} %get-tuple-element.11, pred[384,3072]{0,1:T(8,128)(4,1)S(1)} %get-tuple-element.6), kind=kLoop, calls=%fused_computation.9 | loop fusion | flops 66054912 | bytes 67282944 | tf_op jit(solution)/shard_map/reduce_sum | solution.py:40
  218.5 25.8 %fusion.35 = bf16[2,384,1,7,128]{1,4,3,0,2:T(8,128)(2,1)S(1)} fusion(f32[2,3072,384,7]{2,1,3,0:T(8,128)} %get-tuple-element.14, f32[2,7,384]{2,1,0:T(8,128)S(1)} %get-tuple-element.13, pred[384,3072]{0,1:T(8,128)(4,1)S(1)} %get-tuple-element.5, bf16[2,3072,128]{2,1,0:T(8,128)(2,1)} %all-gather.8.cloned.1.call-done, f32[2,384,7]{1,2,0:T(8,128)S(1)} %bitcast.203), kind=kOutput, calls=%fused_computation.48 | convolution fusion | flops 4295294976 | bytes 70232064 | tf_op jit(solution)/shard_map/bhgqk,bkhd->bqhgd/dot_general | solution.py:41
  244.4 25.0 %fusion.34 = bf16[2,384,1,7,128]{1,4,3,0,2:T(8,128)(2,1)S(1)} fusion(f32[2,3072,384,7]{2,1,3,0:T(8,128)} %get-tuple-element.12, f32[2,7,384]{2,1,0:T(8,128)S(1)} %get-tuple-element.11, pred[384,3072]{0,1:T(8,128)(4,1)S(1)} %get-tuple-element.6, bf16[2,3072,128]{2,1,0:T(8,128)(2,1)S(1)} %copy-done.10, f32[2,384,7]{1,2,0:T(8,128)S(1)} %bitcast.204), kind=kOutput, calls=%fused_computation.46 | convolution fusion | flops 4295294976 | bytes 70232064 | tf_op jit(solution)/shard_map/bhgqk,bkhd->bqhgd/dot_general | solution.py:41
  269.4 18.2 %convolution_bitcast_fusion = f32[2,768,3584]{2,1,0:T(8,128)} fusion(bf16[7,128,3584]{2,1,0:T(8,128)(2,1)} %param.16, bf16[2,384,1,7,128]{1,4,3,0,2:T(8,128)(2,1)S(1)} %fusion.34, bf16[2,384,1,7,128]{1,4,3,0,2:T(8,128)(2,1)S(1)} %fusion.35), kind=kOutput, calls=%fused_computation.29 | convolution fusion | flops 9870508032 | bytes 31195136 | tf_op jit(solution)/shard_map/bsnd,ndh->bsh/dot_general | solution.py:45
  289.1 1.7 reduce-window.6
  291.7 36.0 %scatter_fusion = s32[2,768]{1,0:T(2,128)S(1)} fusion(s32[2,768]{1,0:T(2,128)S(1)} %broadcast_in_dim.73, s32[768]{0:T(1024)S(1)} %reshape.243, s32[768]{0:T(1024)S(1)} %reshape.245), kind=kCustom, calls=%fused_computation.2 | custom fusion | bytes 15360 | tf_op jit(solution)/shard_map/scatter | solution.py:59
  327.9 115.2 %reduce-scatter.2.cloned.1.call-done = f32[2,192,3584]{2,1,0:T(8,128)} async-done(((f32[2,768,3584]{2,1,0:T(8,128)}), f32[2,192,3584]{2,1,0:T(8,128)}) %reduce-scatter.2.cloned.1.call-update) | async-done | bytes 5505040 | tf_op jit(solution)/shard_map/reduce_scatter | solution.py:46
  443.1 4.2 add_convert_fusion
  447.3 48.6 %gather_fusion = bf16[1536,3584]{1,0:T(8,128)(2,1)} fusion(bf16[2,192,3584]{2,1,0:T(8,128)(2,1)S(1)} %add_convert_fusion, s32[1536]{0:T(1024)S(1)} %reshape.231), kind=kCustom, calls=%fused_computation | custom fusion | bytes 22032384 | tf_op jit(solution)/shard_map/vmap(jit(_take))/gather | solution.py:8
  495.9 5.9 copy_select_fusion
  501.8 244.8 %all_to_all.10 = bf16[2,16,48,3584]{3,2,0,1:T(8,128)(2,1)S(1)} all-to-all(bf16[2,16,48,3584]{3,2,0,1:T(8,128)(2,1)S(1)} %copy_select_fusion), channel_id=1, replica_groups=mesh['data'=2,'cp'=4,'tp'=4] {'cp','tp'}, dimensions={1} | all-to-all | bytes 22020096 | tf_op jit(solution)/shard_map/all_to_all | solution.py:61
  746.6 1.7 copy.65
  748.3 34.5 %fusion.18 = f32[2,768,2560]{2,1,0:T(8,128)} fusion(bf16[2,768,3584]{2,1,0:T(8,128)(2,1)S(1)} %bitcast.200, bf16[1,3584,2560]{2,1,0:T(8,128)(2,1)} %param.17), kind=kOutput, calls=%fused_computation.23 | convolution fusion | flops 28185722880 | bytes 45088768 | tf_op jit(solution)/shard_map/bth,hf->btf/dot_general | solution.py:63
  782.8 36.1 %multiply_convert_fusion = bf16[2,768,2560]{2,1,0:T(8,128)(2,1)S(1)} fusion(f32[2,768,2560]{2,1,0:T(8,128)} %fusion.18, bf16[2,768,3584]{2,1,0:T(8,128)(2,1)S(1)} %bitcast.201, bf16[1,3584,2560]{2,1,0:T(8,128)(2,1)} %param.18), kind=kOutput, calls=%fused_computation.25 | convolution fusion | flops 28209315840 | bytes 52953088 | tf_op jit(solution)/shard_map/bth,hf->btf/dot_general | solution.py:64
  818.9 32.7 %fusion.22 = bf16[2,768,3584]{2,1,0:T(8,128)(2,1)S(1)} fusion(bf16[2,768,2560]{2,1,0:T(8,128)(2,1)S(1)} %multiply_convert_fusion, bf16[1,2560,3584]{2,1,0:T(8,128)(2,1)} %param.19), kind=kOutput, calls=%fused_computation.30 | convolution fusion | flops 28191227904 | bytes 37224448 | tf_op jit(solution)/shard_map/btf,fh->bth/dot_general | solution.py:66
  851.5 4.8 copy.66
  856.3 6.3 all-to-all-start.1
  863.1 238.3 %all-to-all-done.1 = bf16[2,16,48,3584]{3,2,0,1:T(8,128)(2,1)} async-done(((bf16[2,16,48,3584]{3,2,0,1:T(8,128)(2,1)}), bf16[2,16,48,3584]{3,2,0,1:T(8,128)(2,1)}, u32[]{:S(2)}, u32[]{:S(2)}) %all-to-all-start.1) | async-done | bytes 11010080 | tf_op jit(solution)/shard_map/all_to_all | solution.py:67
  1101.4 9.5 copy.67
  1110.9 19.4 %gather_fusion.1 = bf16[768,3584]{1,0:T(8,128)(2,1)} fusion(bf16[2,768,3584]{2,1,0:T(8,128)(2,1)} %bitcast.198, s32[768]{0:T(1024)S(1)} %reshape.237), kind=kCustom, calls=%fused_computation.1 | custom fusion | bytes 11016192 | tf_op jit(solution)/shard_map/vmap(jit(_take))/gather | solution.py:8
  1130.4 11.5 gather.15
  1141.9 3.5 copy_select_fusion.1
  1145.4 2.9 fusion.31
  (69 shorter events, 4.1 us)
Async XLA Ops:
  6.5 76.7 %copy-start = (bf16[3584,1,128]{2,0,1:T(8,128)(2,1)S(1)}, bf16[3584,1,128]{2,0,1:T(8,128)(2,1)}, u32[]{:S(2)}) copy-start(bf16[3584,1,128]{2,0,1:T(8,128)(2,1)} %param.14) | copy-start | bytes 2752516
  6.5 85.0 %copy-start.11 = (bf16[3584,1,128]{2,0,1:T(8,128)(2,1)S(1)}, bf16[3584,1,128]{2,0,1:T(8,128)(2,1)}, u32[]{:S(2)}) copy-start(bf16[3584,1,128]{2,0,1:T(8,128)(2,1)} %param.15) | copy-start | bytes 2752516
  6.5 76.6 %all-gather.6.cloned.1.call-start = ((), (), s32[]{:S(2)}) async-start(), calls=%async_computation.3 | async-start | bytes 13762560 | tf_op jit(solution)/shard_map/all_gather | solution.py:20
  7.3 118.2 %all-gather.10.cloned.1.call-start = ((), (), s32[]{:S(2)}) async-start(), calls=%async_computation.6 | async-start | bytes 1966080 | tf_op jit(solution)/shard_map/all_gather | solution.py:25
  89.8 128.7 %all-gather.8.cloned.1.call-start = ((), (), s32[]{:S(2)}) async-start(), calls=%async_computation.5 | async-start | bytes 1966080 | tf_op jit(solution)/shard_map/all_gather | solution.py:26
  98.2 344.9 %reduce-scatter.2.cloned.1.call-start = ((), (), s32[]{:S(2)}) async-start(), calls=%async_computation.4 | async-start | bytes 27525120 | tf_op jit(solution)/shard_map/reduce_scatter | solution.py:46
  218.5 25.9 %copy-start.10 = (bf16[2,3072,128]{2,1,0:T(8,128)(2,1)S(1)}, bf16[2,3072,128]{2,1,0:T(8,128)(2,1)}, u32[]{:S(2)}) copy-start(bf16[2,3072,128]{2,1,0:T(8,128)(2,1)} %all-gather.8.cloned.1.call-done) | copy-start | bytes 4718596
  287.6 0.7 copy-start.4
  291.1 0.6 copy-start.6
  447.3 48.6 %copy-start.2 = (bf16[2,192,3584]{2,1,0:T(8,128)(2,1)}, bf16[2,192,3584]{2,1,0:T(8,128)(2,1)S(1)}, u32[]{:S(2)}) copy-start(bf16[2,192,3584]{2,1,0:T(8,128)(2,1)S(1)} %add_convert_fusion) | copy-start | bytes 8257540
  856.3 6.4 copy-start.7
  856.3 6.6 copy-start.8
  856.3 6.7 copy-start.5
  856.3 6.7 copy-start.9
  856.3 245.1 %all-to-all-start.1 = ((bf16[2,16,48,3584]{3,2,0,1:T(8,128)(2,1)}), bf16[2,16,48,3584]{3,2,0,1:T(8,128)(2,1)}, u32[]{:S(2)}, u32[]{:S(2)}) async-start(bf16[2,16,48,3584]{3,2,0,1:T(8,128)(2,1)} %copy.66), calls=%async_computation.2 | async-start | bytes 22020096 | tf_op jit(solution)/shard_map/all_to_all | solution.py:67
  1130.4 17.9 %copy-start.1 = (bf16[3584,1,128]{2,0,1:T(8,128)(2,1)S(1)}, bf16[3584,1,128]{2,0,1:T(8,128)(2,1)}, u32[]{:S(2)}) copy-start(bf16[3584,1,128]{2,0,1:T(8,128)(2,1)} %param.14) | copy-start | bytes 2752516
  1141.9 3.5 copy-start.3
Sparse Core Ops, SparseCore 0:
  8.9 74.2 all-gather.5
  89.9 35.5 all-gather.9
  127.1 35.7 all-gather.7
  287.7 155.3 reduce-scatter.1
where the time goes:
time: 1160 us
  waiting for transfers between devices  440 us (38%)
  matrix products  253 us (22%)
  blocking collectives  245 us (21%)
  local copies, waits for them, and re-layouts  134 us (12%)
  other arithmetic  62.7 us (5%)
  between operations  13.7 us (1%)
    all_to_all x1, blocking collectives, dispatch_experts(): recv_buf = lax.all_to_all(send_buf, ('cp', 'tp'), 1, 1, tiled=True)  245 us
    all_to_all x1, waiting for transfers between devices, dispatch_experts(): lax.all_to_all(expert_out.reshape(n_micro, experts, capacity, hidden), ('...  238 us
    reduce_scatter x1, waiting for transfers between devices, attend_local(): attn_sum = lax.psum_scatter(partial, 'tp', scatter_dimension=1, tiled=True)  115 us
    gather x4, local copies, waits for them, and re-layouts, pick_rows(): return jnp.take(row_table, row_ids, axis=0, mode='fill', fill_value=0)  79.5 us
    all_gather x1, waiting for transfers between devices, attend_local(): x_half = lax.all_gather(act_in, 'tp', axis=1, tiled=True)  75.9 us
    dot_general x2, matrix products, attend_local(): jnp.einsum('bqhgd,bkhd->bhgqk', q_part, key_all, preferred_element_type=j...  51 us
    dot_general x2, matrix products, attend_local(): jnp.einsum('bhgqk,bkhd->bqhgd', exp_scores.astype(jnp.bfloat16), value_al...  50.9 us
    reduce_sum x2, other arithmetic, attend_local(): row_sum = jnp.sum(exp_scores, axis=-1)  42 us
  transfers between devices with their start and end apart: 5, of which 4 were waited for; matrix products, arithmetic and copies ran while one was open for 14% of the time, Pallas kernels for 0%

commit v1 on v0

v1 whole, which is shorter than its diff:
```python
import jax
import jax.numpy as jnp
from jax import lax
from jax.experimental import pallas as pl
from jax.experimental.pallas import tpu as pltpu
from jax.sharding import PartitionSpec as P

F32, BF16 = jnp.float32, jnp.bfloat16


def attend_kernel(cp_size, heads, rank_ref, q_ref, kv_ref, o_ref, vt_ref, acc_ref):
    piece, dim = q_ref.shape[0] // 2, q_ref.shape[1] // heads
    pieces = 2 * cp_size
    scale = dim ** -0.5
    for j in range(pieces):
        owner, half = (j, 0) if j < cp_size else (pieces - 1 - j, 1)
        vt_ref[j] = kv_ref[owner, half * piece:(half + 1) * piece, dim:].T
    rank = rank_ref[0]

    def keys_of(j):
        owner = jnp.where(j < cp_size, j, pieces - 1 - j)
        start = jnp.where(j < cp_size, 0, piece)
        return kv_ref[owner, pl.ds(pl.multiple_of(start, piece), piece), 0:dim]

    for half in range(2):
        last = rank if half == 0 else pieces - 1 - rank
        rows = slice(half * piece, (half + 1) * piece)
        for first in range(0, heads, 2):
            group = range(first, min(first + 2, heads))
            cols = len(group) * piece
            qt = jnp.concatenate([q_ref[rows, n * dim:(n + 1) * dim].T for n in group], axis=1)
            key_ix = lax.broadcasted_iota(jnp.int32, (piece, piece), 0)
            query_ix = lax.broadcasted_iota(jnp.int32, (piece, piece), 1)
            keep = key_ix <= query_ix
            if len(group) == 2:
                keep = jnp.concatenate([keep, keep], axis=1)
            s = jnp.dot(keys_of(last), qt, preferred_element_type=F32) * scale
            s = jnp.where(keep, s, -jnp.inf)
            peak = jnp.max(s, axis=0, keepdims=True)
            e = jnp.exp(s - peak)
            total = jnp.sum(e, axis=0, keepdims=True)
            acc_ref[:, 0:cols] = jnp.dot(vt_ref[last], e.astype(BF16), preferred_element_type=F32)

            def step(j, carry):
                peak, total = carry
                s = jnp.dot(keys_of(j), qt, preferred_element_type=F32) * scale
                new_peak = jnp.maximum(peak, jnp.max(s, axis=0, keepdims=True))
                e = jnp.exp(s - new_peak)
                shrink = jnp.exp(peak - new_peak)
                total = total * shrink + jnp.sum(e, axis=0, keepdims=True)
                acc_ref[:, 0:cols] = acc_ref[:, 0:cols] * shrink + jnp.dot(vt_ref[j], e.astype(BF16), preferred_element_type=F32)
                return new_peak, total

            peak, total = lax.fori_loop(0, last, step, (peak, total))
            out = (acc_ref[:, 0:cols] / total).T.astype(BF16)
            for k, n in enumerate(group):
                o_ref[rows, n * dim:(n + 1) * dim] = out[k * piece:(k + 1) * piece]


def attend(rank, q, kv, cp_size, heads):
    rows, width = q.shape
    dim = width // heads
    vmem = pl.BlockSpec(memory_space=pltpu.VMEM)
    pairs = heads * (rows // 2) ** 2 * (2 * cp_size + 1)
    return pl.pallas_call(
        lambda *refs: attend_kernel(cp_size, heads, *refs),
        out_shape=jax.ShapeDtypeStruct(q.shape, BF16),
        in_specs=[pl.BlockSpec(memory_space=pltpu.SMEM), vmem, vmem],
        out_specs=vmem,
        scratch_shapes=[pltpu.VMEM((2 * cp_size, dim, rows // 2), BF16), pltpu.VMEM((dim, rows), F32)],
        cost_estimate=pl.CostEstimate(flops=6 * dim * pairs, bytes_accessed=4 * q.size + 2 * kv.size, transcendentals=pairs),
        compiler_params=pltpu.CompilerParams(vmem_limit_bytes=24 * 2 ** 20),
    )(rank, q, kv)


def dot(a, b, out=F32):
    return jnp.dot(a, b, preferred_element_type=F32).astype(out)


def solution(mesh):
    cp_size = mesh.shape['cp']
    tp_size = mesh.shape['tp']
    experts = cp_size * tp_size
    row_spec = P(None, ('data', 'cp', 'tp'), None)
    head_spec = P(None, 'tp', None)
    out_spec = P('tp', None, None)
    expert_spec = P(('cp', 'tp'), None, None)
    group = ('cp', 'tp')

    def device_step(act_in, route_ids, route_gates, w_query, w_key, w_value, w_out, w_gate, w_up, w_down):
        n_micro, tokens, hidden = act_in.shape
        heads, dim = w_query.shape[1], w_query.shape[2]
        rank = lax.axis_index('cp')[None].astype(jnp.int32)
        wq = w_query.reshape(hidden, heads * dim)
        wkv = jnp.concatenate([w_key.reshape(hidden, dim), w_value.reshape(hidden, dim)], axis=1)
        wo = w_out.reshape(heads * dim, hidden)

        choices = 2 * tokens
        capacity = 2 * choices // experts
        flat_ids = route_ids.reshape(n_micro, choices)
        hits = (flat_ids[..., None] == jnp.arange(experts)).astype(jnp.int32)
        slot_rank = jnp.cumsum(hits, axis=1) - 1
        slots = (flat_ids * capacity + jnp.sum(slot_rank * hits, axis=-1)).reshape(n_micro, tokens, 2)
        slot_ix = jnp.arange(experts * capacity)

        mids = []
        for b in range(n_micro):
            x_half = lax.all_gather(act_in[b], 'tp', axis=0, tiled=True)
            kv = dot(x_half, wkv, BF16)
            q = dot(x_half, wq, BF16)
            kv_all = lax.all_gather(kv, 'cp', axis=0)
            o = attend(rank, q, kv_all, cp_size, heads)
            attn_sum = lax.psum_scatter(dot(o, wo), 'tp', scatter_dimension=0, tiled=True)
            mids.append((act_in[b].astype(F32) + attn_sum).astype(BF16))

        outs = []
        for b in range(n_micro):
            mid = mids[b]
            pick = ((slots[b, :, 0][None, :] == slot_ix[:, None]) | (slots[b, :, 1][None, :] == slot_ix[:, None])).astype(BF16)
            send = dot(pick, mid, BF16)
            expert_in = lax.all_to_all(send, group, 0, 0, tiled=True)
            gate_act = dot(expert_in, w_gate[0])
            up_act = dot(expert_in, w_up[0])
            mixed = (jax.nn.silu(gate_act) * up_act).astype(BF16)
            expert_out = dot(mixed, w_down[0], BF16)
            back = lax.all_to_all(expert_out, group, 0, 0, tiled=True)
            z0 = dot((slots[b, :, 0][:, None] == slot_ix[None, :]).astype(BF16), back)
            z1 = dot((slots[b, :, 1][:, None] == slot_ix[None, :]).astype(BF16), back)
            gates = route_gates[b]
            outs.append((mid.astype(F32) + gates[:, 0:1] * z0 + gates[:, 1:2] * z1).astype(BF16))
        return jnp.stack(outs)

    return jax.shard_map(device_step, mesh=mesh, in_specs=(row_spec, row_spec, row_spec, head_spec, head_spec, head_spec, out_spec, expert_spec, expert_spec, expert_spec), out_specs=row_spec, check_vma=False)
```

time: 1160 us -> 804 us (0.69)
  blocking collectives: 245 us -> 0 us
  local copies, waits for them, and re-layouts: 134 us -> 18.2 us
  other arithmetic: 62.7 us -> 3.63 us
  matrix products: 253 us -> 202 us
  Pallas kernels: 0 us -> 48.1 us
  waiting for transfers between devices: 440 us -> 483 us
  starting transfers between devices: 6.77 us -> 25.8 us
    all_to_all x1 -> x0, blocking collectives: 245 us -> none  [dispatch_experts(): recv_buf = lax.all_to_all(send_buf, ('cp', 'tp'), 1, 1, tiled=True)]
    gather x4 -> x0, local copies, waits for them, and re-layouts: 79.5 us -> none  [pick_rows(): return jnp.take(row_table, row_ids, axis=0, mode='fill', fill_value=0)]
    dot_general x11 -> x18, matrix products: 253 us -> 202 us  [dot(): return jnp.dot(a, b, preferred_element_type=F32).astype(out)]
    pallas_call x0 -> x2, Pallas kernels: none -> 48.1 us  [attend(): pl.pallas_call(lambda *refs: attend_kernel(cp_size, heads, *refs), out_sh...]
    reduce_sum x3 -> x1, other arithmetic: 42.1 us -> 0.11 us  [device_step(): jnp.sum(slot_rank * hits, axis=-1)]
    reduce_scatter x1 -> x2, waiting for transfers between devices: 115 us -> 156 us  [device_step(): lax.psum_scatter(dot(o, wo), 'tp', scatter_dimension=0, tiled=True)]
    scatter x1 -> x0, local copies, waits for them, and re-layouts: 36 us -> none  [dispatch_experts(): jnp.full((n_micro, experts * capacity), tokens, jnp.int32)]
    all_to_all x1 -> x4, starting transfers between devices: 6.35 us -> 25.6 us  [the longest x2 15.8 us: device_step(): expert_in = lax.all_to_all(send, group, 0, 0, tiled=True)]
  transfers between devices with their start and end apart: 5 -> 10, of which waited for: 4 -> 8; matrix products, arithmetic and copies ran while one was open for 14% -> 26% of each run, Pallas kernels for 0% -> 6%
where the time goes in v1:
time: 804 us; the launch traced here: 795 us
  waiting for transfers between devices  483 us (60%)
  matrix products  202 us (25%)
  Pallas kernels  48.1 us (6%)
  starting transfers between devices  25.8 us (3%)
  local copies, waits for them, and re-layouts  18.2 us (2%)
  between operations  14.2 us (2%)
    dot_general x18, matrix products, dot(): return jnp.dot(a, b, preferred_element_type=F32).astype(out)  202 us
    all_to_all x2, waiting for transfers between devices, device_step(): back = lax.all_to_all(expert_out, group, 0, 0, tiled=True)  172 us
    reduce_scatter x2, waiting for transfers between devices, device_step(): lax.psum_scatter(dot(o, wo), 'tp', scatter_dimension=0, tiled=True)  156 us
    all_gather x2, waiting for transfers between devices, device_step(): x_half = lax.all_gather(act_in[b], 'tp', axis=0, tiled=True)  70.7 us
    all_to_all x2, waiting for transfers between devices, device_step(): expert_in = lax.all_to_all(send, group, 0, 0, tiled=True)  60.8 us
    pallas_call x2, Pallas kernels, attend(): pl.pallas_call(lambda *refs: attend_kernel(cp_size, heads, *refs), out_sh...  48.1 us
    all_gather x2, waiting for transfers between devices, device_step(): kv_all = lax.all_gather(kv, 'cp', axis=0)  22.4 us
  transfers between devices with their start and end apart: 10, of which 8 were waited for; matrix products, arithmetic and copies ran while one was open for 26% of the time, Pallas kernels for 6%

profile of v1, /device:TPU:13, one launch (start us, length us, event | category | flops | bytes accessed | tf_op | source)
XLA Modules:
  0.0 794.8 jit_solution(6391385278702935484)
XLA Ops:
  11.0 41.8 %all-gather.13.cloned.1.call-done = bf16[1,768,3584]{2,1,0:T(8,128)(2,1)} async-done(((bf16[1,192,3584]{2,1,0:T(8,128)(2,1)}), bf16[1,768,3584]{2,1,0:T(8,128)(2,1)}) %all-gather.13.cloned.1.call-update) | async-done | bytes 5505040 | tf_op jit(solution)/shard_map/all_gather | solution.py:108
  52.8 5.0 fusion.58
  57.9 9.5 %copy.35 = bf16[3584,7,128]{0,2,1:T(8,128)(2,1)} copy(bf16[3584,7,128]{2,0,1:T(8,128)(2,1)} %param.13) | data formatting | bytes 12845056 | tf_op args[3]
  67.4 28.9 %all-gather.9.cloned.1.call-done = bf16[1,768,3584]{2,1,0:T(8,128)(2,1)} async-done(((bf16[1,192,3584]{2,1,0:T(8,128)(2,1)}), bf16[1,768,3584]{2,1,0:T(8,128)(2,1)}) %all-gather.9.cloned.1.call-update) | async-done | bytes 5505040 | tf_op jit(solution)/shard_map/all_gather | solution.py:108
  96.3 4.9 fusion.61
  101.3 9.8 %fusion.49.refs_1_ = bf16[768,896]{1,0:T(8,128)(2,1)S(1)} fusion(bf16[3584,896]{0,1:T(8,128)(2,1)} %bitcast.143, bf16[1,768,3584]{2,1,0:T(8,128)(2,1)} %all-gather.13.cloned.1.call-done), kind=kOutput, calls=%fused_computation.47 | convolution fusion | flops 4933189632 | bytes 13303808 | tf_op jit(solution)/shard_map/dot_general | solution.py:77
  111.0 22.4 %all-gather.15.cloned.1.call-done = bf16[3072,256]{0,1:T(8,128)(2,1)} async-done(((bf16[768,256]{0,1:T(8,128)(2,1)}), bf16[3072,256]{0,1:T(8,128)(2,1)}) %all-gather.15.cloned.1.call-update) | async-done | bytes 1572880 | tf_op jit(solution)/shard_map/all_gather | solution.py:111
  135.1 23.9 %shard_map.101 = bf16[768,896]{1,0:T(8,128)(2,1)S(1)} custom-call(s32[1]{0:T(128)} %bitcast.1.refs_0_, bf16[768,896]{1,0:T(8,128)(2,1)S(1)} %fusion.49.refs_1_, bf16[4,768,256]{2,1,0:T(8,128)(2,1)S(1)} %bitcast.140), custom_call_target="tpu_custom_call" | custom-call | flops 7134511104 | bytes 4325376 | tf_op jit(solution)/shard_map/pallas_call | solution.py:65
  159.1 11.4 %fusion.94 = f32[768,3584]{1,0:T(8,128)} fusion(bf16[768,896]{1,0:T(8,128)(2,1)S(1)} %shard_map.101, bf16[896,3584]{1,0:T(8,128)(2,1)} %bitcast.159), kind=kOutput, calls=%fused_computation.93 | convolution fusion | flops 4932501504 | bytes 18808832 | tf_op jit(solution)/shard_map/dot_general | solution.py:77
  170.6 9.8 %fusion.46.refs_1_ = bf16[768,896]{1,0:T(8,128)(2,1)S(1)} fusion(bf16[3584,896]{0,1:T(8,128)(2,1)} %bitcast.144, bf16[1,768,3584]{2,1,0:T(8,128)(2,1)} %all-gather.9.cloned.1.call-done), kind=kOutput, calls=%fused_computation.46 | convolution fusion | flops 4933189632 | bytes 13303808 | tf_op jit(solution)/shard_map/dot_general | solution.py:77
  182.1 24.1 %shard_map.100 = bf16[768,896]{1,0:T(8,128)(2,1)S(1)} custom-call(s32[1]{0:T(128)} %bitcast.1.refs_0_, bf16[768,896]{1,0:T(8,128)(2,1)S(1)} %fusion.46.refs_1_, bf16[4,768,256]{2,1,0:T(8,128)(2,1)S(1)} %bitcast.139), custom_call_target="tpu_custom_call" | custom-call | flops 7134511104 | bytes 4325376 | tf_op jit(solution)/shard_map/pallas_call | solution.py:65
  206.2 11.4 %fusion.93 = f32[768,3584]{1,0:T(8,128)} fusion(bf16[768,896]{1,0:T(8,128)(2,1)S(1)} %shard_map.100, bf16[896,3584]{1,0:T(8,128)(2,1)} %bitcast.160), kind=kOutput, calls=%fused_computation.92 | convolution fusion | flops 4932501504 | bytes 18808832 | tf_op jit(solution)/shard_map/dot_general | solution.py:77
  221.1 38.1 %reduce-scatter.5.cloned.1.call-done = f32[192,3584]{1,0:T(8,128)} async-done(((f32[768,3584]{1,0:T(8,128)}), f32[192,3584]{1,0:T(8,128)}) %reduce-scatter.5.cloned.1.call-update) | async-done | bytes 2752528 | tf_op jit(solution)/shard_map/reduce_scatter | solution.py:113
  259.3 5.8 convolution_convert_fusion
  265.1 6.6 all-to-all-start.2
  271.7 118.3 %reduce-scatter.3.cloned.1.call-done = f32[192,3584]{1,0:T(8,128)} async-done(((f32[768,3584]{1,0:T(8,128)}), f32[192,3584]{1,0:T(8,128)}) %reduce-scatter.3.cloned.1.call-update) | async-done | bytes 2752528 | tf_op jit(solution)/shard_map/reduce_scatter | solution.py:113
  390.0 5.8 convolution_convert_fusion.1
  395.8 9.2 %all-to-all-start = ((bf16[16,48,3584]{2,1,0:T(8,128)(2,1)}), bf16[16,48,3584]{2,1,0:T(8,128)(2,1)}, u32[]{:S(2)}, u32[]{:S(2)}) async-start(bf16[16,48,3584]{2,1,0:T(8,128)(2,1)} %bitcast.141), calls=%async_computation.1 | async-start | bytes 11010048 | tf_op jit(solution)/shard_map/all_to_all | solution.py:121
  405.0 19.7 %fusion.8 = f32[768,2560]{1,0:T(8,128)S(1)} fusion(bf16[768,3584]{1,0:T(8,128)(2,1)} %bitcast.33, bf16[1,3584,2560]{2,1,0:T(8,128)(2,1)} %param.17), kind=kOutput, calls=%fused_computation.8 | convolution fusion | flops 14092861440 | bytes 31719424 | tf_op jit(solution)/shard_map/dot_general | solution.py:77
  424.7 20.1 %multiply_convert_fusion.clone.2 = bf16[768,2560]{1,0:T(8,128)(2,1)S(1)} fusion(f32[768,2560]{1,0:T(8,128)S(1)} %fusion.8, bf16[768,3584]{1,0:T(8,128)(2,1)} %bitcast.33, bf16[1,3584,2560]{2,1,0:T(8,128)(2,1)} %param.18), kind=kOutput, calls=%fused_computation.12.clone.clone.clone | convolution fusion | flops 14104657920 | bytes 35651584 | tf_op jit(solution)/shard_map/dot_general | solution.py:77
  444.8 19.9 %fusion.15 = bf16[768,3584]{1,0:T(8,128)(2,1)} fusion(bf16[1,2560,3584]{2,1,0:T(8,128)(2,1)} %param.19, bf16[768,2560]{1,0:T(8,128)(2,1)S(1)} %multiply_convert_fusion.clone.2), kind=kOutput, calls=%fused_computation.17 | convolution fusion | flops 14095613952 | bytes 27787264 | tf_op jit(solution)/shard_map/dot_general | solution.py:77
  464.8 60.8 %all-to-all-done = bf16[16,48,3584]{2,1,0:T(8,128)(2,1)} async-done(((bf16[16,48,3584]{2,1,0:T(8,128)(2,1)}), bf16[16,48,3584]{2,1,0:T(8,128)(2,1)}, u32[]{:S(2)}, u32[]{:S(2)}) %all-to-all-start) | async-done | bytes 5505056 | tf_op jit(solution)/shard_map/all_to_all | solution.py:121
  525.6 4.8 all-to-all-start.3
  530.4 19.7 %fusion.10 = f32[768,2560]{1,0:T(8,128)S(1)} fusion(bf16[768,3584]{1,0:T(8,128)(2,1)} %bitcast.16, bf16[1,3584,2560]{2,1,0:T(8,128)(2,1)} %param.17), kind=kOutput, calls=%fused_computation.10 | convolution fusion | flops 14092861440 | bytes 31719424 | tf_op jit(solution)/shard_map/dot_general | solution.py:77
  550.1 20.1 %multiply_convert_fusion.1.clone.4 = bf16[768,2560]{1,0:T(8,128)(2,1)S(1)} fusion(f32[768,2560]{1,0:T(8,128)S(1)} %fusion.10, bf16[768,3584]{1,0:T(8,128)(2,1)} %bitcast.16, bf16[1,3584,2560]{2,1,0:T(8,128)(2,1)} %param.18), kind=kOutput, calls=%fused_computation.13.clone.clone.clone.1 | convolution fusion | flops 14104657920 | bytes 35651584 | tf_op jit(solution)/shard_map/dot_general | solution.py:77
  570.2 20.0 %fusion.12 = bf16[768,3584]{1,0:T(8,128)(2,1)} fusion(bf16[1,2560,3584]{2,1,0:T(8,128)(2,1)} %param.19, bf16[768,2560]{1,0:T(8,128)(2,1)S(1)} %multiply_convert_fusion.1.clone.4), kind=kOutput, calls=%fused_computation.16 | convolution fusion | flops 14095613952 | bytes 27787264 | tf_op jit(solution)/shard_map/dot_general | solution.py:77
  590.2 60.9 %all-to-all-done.3 = bf16[16,48,3584]{2,1,0:T(8,128)(2,1)} async-done(((bf16[16,48,3584]{2,1,0:T(8,128)(2,1)}), bf16[16,48,3584]{2,1,0:T(8,128)(2,1)}, u32[]{:S(2)}, u32[]{:S(2)}) %all-to-all-start.3) | async-done | bytes 5505056 | tf_op jit(solution)/shard_map/all_to_all | solution.py:126
  651.1 5.1 all-to-all-start.1
  656.3 4.7 fusion.36
  661.0 5.0 fusion.41
  666.0 110.9 %all-to-all-done.1 = bf16[16,48,3584]{2,1,0:T(8,128)(2,1)} async-done(((bf16[16,48,3584]{2,1,0:T(8,128)(2,1)}), bf16[16,48,3584]{2,1,0:T(8,128)(2,1)}, u32[]{:S(2)}, u32[]{:S(2)}) %all-to-all-start.1) | async-done | bytes 5505056 | tf_op jit(solution)/shard_map/all_to_all | solution.py:126
  777.0 4.7 fusion.34
  (66 shorter events, 17.4 us)
Async XLA Ops:
  6.5 46.3 %copy-start.13 = (bf16[3584,1,128]{2,0,1:T(8,128)(2,1)S(1)}, bf16[3584,1,128]{2,0,1:T(8,128)(2,1)}, u32[]{:S(2)}) copy-start(bf16[3584,1,128]{2,0,1:T(8,128)(2,1)} %param.15) | copy-start | bytes 2752516
  6.5 46.3 %copy-start.14 = (bf16[3584,1,128]{2,0,1:T(8,128)(2,1)S(1)}, bf16[3584,1,128]{2,0,1:T(8,128)(2,1)}, u32[]{:S(2)}) copy-start(bf16[3584,1,128]{2,0,1:T(8,128)(2,1)} %param.14) | copy-start | bytes 2752516
  6.5 46.3 %all-gather.13.cloned.1.call-start = ((), (), s32[]{:S(2)}) async-start(), calls=%async_computation.10 | async-start | bytes 6881280 | tf_op jit(solution)/shard_map/all_gather | solution.py:108
  10.2 86.1 %all-gather.9.cloned.1.call-start = ((), (), s32[]{:S(2)}) async-start(), calls=%async_computation.8 | async-start | bytes 6881280 | tf_op jit(solution)/shard_map/all_gather | solution.py:108
  11.0 122.4 %all-gather.15.cloned.1.call-start = ((), (), s32[]{:S(2)}) async-start(), calls=%async_computation.11 | async-start | bytes 1966080 | tf_op jit(solution)/shard_map/all_gather | solution.py:111
  57.8 122.5 %all-gather.11.cloned.1.call-start = ((), (), s32[]{:S(2)}) async-start(), calls=%async_computation.9 | async-start | bytes 1966080 | tf_op jit(solution)/shard_map/all_gather | solution.py:111
  101.2 158.0 %reduce-scatter.5.cloned.1.call-start = ((), (), s32[]{:S(2)}) async-start(), calls=%async_computation.7 | async-start | bytes 13762560 | tf_op jit(solution)/shard_map/reduce_scatter | solution.py:113
  170.5 219.5 %reduce-scatter.3.cloned.1.call-start = ((), (), s32[]{:S(2)}) async-start(), calls=%async_computation.6 | async-start | bytes 13762560 | tf_op jit(solution)/shard_map/reduce_scatter | solution.py:113
  217.6 0.7 copy-start.7
  217.6 41.7 %copy-start = (bf16[2,192,3584]{2,1,0:T(8,128)(2,1)S(1)}, bf16[2,192,3584]{2,1,0:T(8,128)(2,1)}, u32[]{:S(2)}) copy-start(bf16[2,192,3584]{2,1,0:T(8,128)(2,1)} %param.10) | copy-start | bytes 8257540
  221.1 44.0 %copy-start.5 = (s32[1,192,1]{1,2,0:T(1,128)}, s32[1,192,1]{1,2,0:T(1,128)S(1)}, u32[]{:S(2)}) copy-start(s32[1,192,1]{1,2,0:T(1,128)S(1)} %get-tuple-element.11) | copy-start | bytes 2308
  221.1 44.0 %copy-start.10 = (s32[1,192,1]{1,2,0:T(1,128)}, s32[1,192,1]{1,2,0:T(1,128)S(1)}, u32[]{:S(2)}) copy-start(s32[1,192,1]{1,2,0:T(1,128)S(1)} %get-tuple-element.10) | copy-start | bytes 2308
  221.1 168.9 %copy-start.3 = (s32[1,192,1]{1,2,0:T(1,128)}, s32[1,192,1]{1,2,0:T(1,128)S(1)}, u32[]{:S(2)}) copy-start(s32[1,192,1]{1,2,0:T(1,128)S(1)} %get-tuple-element.9) | copy-start | bytes 2308
  221.1 168.9 %copy-start.8 = (s32[1,192,1]{1,2,0:T(1,128)}, s32[1,192,1]{1,2,0:T(1,128)S(1)}, u32[]{:S(2)}) copy-start(s32[1,192,1]{1,2,0:T(1,128)S(1)} %get-tuple-element.12) | copy-start | bytes 2308
  265.1 130.7 %all-to-all-start.2 = ((bf16[16,48,3584]{2,1,0:T(8,128)(2,1)}), bf16[16,48,3584]{2,1,0:T(8,128)(2,1)}, u32[]{:S(2)}, u32[]{:S(2)}) async-start(bf16[16,48,3584]{2,1,0:T(8,128)(2,1)} %bitcast.142), calls=%async_computation.4 | async-start | bytes 11010048 | tf_op jit(solution)/shard_map/all_to_all | solution.py:121
  395.8 129.8 %all-to-all-start = ((bf16[16,48,3584]{2,1,0:T(8,128)(2,1)}), bf16[16,48,3584]{2,1,0:T(8,128)(2,1)}, u32[]{:S(2)}, u32[]{:S(2)}) async-start(bf16[16,48,3584]{2,1,0:T(8,128)(2,1)} %bitcast.141), calls=%async_computation.1 | async-start | bytes 11010048 | tf_op jit(solution)/shard_map/all_to_all | solution.py:121
  525.6 125.6 %all-to-all-start.3 = ((bf16[16,48,3584]{2,1,0:T(8,128)(2,1)}), bf16[16,48,3584]{2,1,0:T(8,128)(2,1)}, u32[]{:S(2)}, u32[]{:S(2)}) async-start(bf16[16,48,3584]{2,1,0:T(8,128)(2,1)} %bitcast.146), calls=%async_computation.5 | async-start | bytes 11010048 | tf_op jit(solution)/shard_map/all_to_all | solution.py:126
  651.1 5.1 copy-start.12
  651.1 5.1 copy-start.1
  651.1 5.1 copy-start.6
  651.1 125.8 %all-to-all-start.1 = ((bf16[16,48,3584]{2,1,0:T(8,128)(2,1)}), bf16[16,48,3584]{2,1,0:T(8,128)(2,1)}, u32[]{:S(2)}, u32[]{:S(2)}) async-start(bf16[16,48,3584]{2,1,0:T(8,128)(2,1)} %bitcast.145), calls=%async_computation.2 | async-start | bytes 11010048 | tf_op jit(solution)/shard_map/all_to_all | solution.py:126
  656.2 4.8 copy-start.11
  661.0 116.0 %copy-start.4 = (s32[1,192,1]{1,2,0:T(1,128)S(1)}, s32[1,192,1]{1,2,0:T(1,128)}, u32[]{:S(2)}) copy-start(s32[1,192,1]{1,2,0:T(1,128)} %copy-done.3) | copy-start | bytes 2308
  777.0 4.7 copy-start.9
  781.7 4.1 copy-start.2
Sparse Core Ops, SparseCore 0:
  10.3 42.4 all-gather.12
  54.4 41.8 all-gather.8
  97.8 35.5 all-gather.14
  134.8 35.7 all-gather.10
  173.1 86.1 reduce-scatter.4
  261.7 128.2 reduce-scatter.2

commit v2 on v1

--- a/solution.py
+++ b/solution.py
@@ -4,6 +4,7 @@
 from jax.experimental import pallas as pl
 from jax.experimental.pallas import tpu as pltpu
 from jax.sharding import PartitionSpec as P
+
 
 F32, BF16 = jnp.float32, jnp.bfloat16
 
@@ -77,6 +78,10 @@
     return jnp.dot(a, b, preferred_element_type=F32).astype(out)
 
 
+def after(value, *first):
+    return lax.optimization_barrier((value,) + first)[0]
+
+
 def solution(mesh):
     cp_size = mesh.shape['cp']
     tp_size = mesh.shape['tp']
@@ -96,38 +101,93 @@
         wo = w_out.reshape(heads * dim, hidden)
 
         choices = 2 * tokens
-        capacity = 2 * choices // experts
-        flat_ids = route_ids.reshape(n_micro, choices)
-        hits = (flat_ids[..., None] == jnp.arange(experts)).astype(jnp.int32)
+        near_n = experts // 2
+        capacity = 4 * choices // experts
+        half_id = lax.axis_index('cp') // (cp_size // 2)
+        swap = [(i, (i + cp_size // 2) % cp_size) for i in range(cp_size)]
+        peer_ids = lax.ppermute(route_ids, 'cp', swap)
+        pair_ids = jnp.concatenate([route_ids, peer_ids], axis=1)
+        peer_gates = lax.ppermute(route_gates, 'cp', swap)
+        near_ids = pair_ids.reshape(n_micro, 2 * choices) - half_id * near_n
+        hits = (near_ids[..., None] == jnp.arange(near_n)).astype(jnp.int32)
         slot_rank = jnp.cumsum(hits, axis=1) - 1
-        slots = (flat_ids * capacity + jnp.sum(slot_rank * hits, axis=-1)).reshape(n_micro, tokens, 2)
-        slot_ix = jnp.arange(experts * capacity)
+        near = jnp.sum(hits, axis=-1) > 0
+        slots = jnp.where(near, near_ids * capacity + jnp.sum(slot_rank * hits, axis=-1), -1).reshape(n_micro, 2 * tokens, 2)
+        near = near.reshape(n_micro, 2 * tokens, 2)
+        slot_ix = jnp.arange(near_n * capacity)
+        halves = [list(range(h * near_n, (h + 1) * near_n)) for h in range(2)]
 
-        mids = []
+        t_rank = lax.axis_index('tp')
+        other_core = [(t, t ^ 1) for t in range(tp_size)]
+        other_chip = [(t, t ^ 2) for t in range(tp_size)]
+
+        def rows_of(o, k):
+            return lax.dynamic_slice_in_dim(o, jnp.bitwise_xor(t_rank, k) * tokens, tokens, axis=0)
+
+        overs, owns, sent = [], [], []
         for b in range(n_micro):
-            x_half = lax.all_gather(act_in[b], 'tp', axis=0, tiled=True)
+            x_own = act_in[b] if b == 0 else after(act_in[b], first_kv)
+            x_half = lax.all_gather(x_own, 'tp', axis=0, tiled=True)
+            x_half = after(x_half, slots, near, peer_gates) if b == 0 else after(x_half, sent[b - 1])
             kv = dot(x_half, wkv, BF16)
-            q = dot(x_half, wq, BF16)
+            if b == 0:
+                first_kv = kv
+            q = dot(after(x_half, kv), wq, BF16)
             kv_all = lax.all_gather(kv, 'cp', axis=0)
             o = attend(rank, q, kv_all, cp_size, heads)
-            attn_sum = lax.psum_scatter(dot(o, wo), 'tp', scatter_dimension=0, tiled=True)
-            mids.append((act_in[b].astype(F32) + attn_sum).astype(BF16))
+            give = dot(jnp.concatenate([rows_of(o, 3), rows_of(o, 1)], axis=0), wo)
+            got = lax.ppermute(give, 'tp', other_core)
+            keep = dot(jnp.concatenate([rows_of(after(o, give), 2), rows_of(after(o, give), 0)], axis=0), wo)
+            sent.append(keep[:tokens] + got[:tokens])
+            overs.append(lax.ppermute(sent[b], 'tp', other_chip))
+            owns.append(keep[tokens:] + got[tokens:])
 
-        outs = []
+        mids, peers = [], []
         for b in range(n_micro):
-            mid = mids[b]
+            over = after(overs[b], sent[-1]) if b == 0 else after(overs[b], mids[b - 1])
+            mids.append((act_in[b].astype(F32) + (owns[b] + over)).astype(BF16))
+            peers.append(lax.ppermute(mids[b], 'cp', swap))
+
+        def pick_of(b, choice):
+            return (slots[b, :, choice][:, None] == slot_ix[None, :]).astype(BF16)
+
+        pairs, sends = [], []
+        for b in range(n_micro):
+            peer = after(peers[b], mids[-1] if b == 0 else sends[b - 1])
+            pairs.append(jnp.concatenate([mids[b], peer], axis=0))
             pick = ((slots[b, :, 0][None, :] == slot_ix[:, None]) | (slots[b, :, 1][None, :] == slot_ix[:, None])).astype(BF16)
-            send = dot(pick, mid, BF16)
-            expert_in = lax.all_to_all(send, group, 0, 0, tiled=True)
+            sends.append(dot(pick, pairs[b], BF16))
+        results = []
+        for b in range(n_micro):
+            expert_in = lax.all_to_all(sends[b], group, 0, 0, tiled=True, axis_index_groups=halves)
+            expert_in = after(expert_in, sends[-1] if b == 0 else results[b - 1])
             gate_act = dot(expert_in, w_gate[0])
             up_act = dot(expert_in, w_up[0])
             mixed = (jax.nn.silu(gate_act) * up_act).astype(BF16)
-            expert_out = dot(mixed, w_down[0], BF16)
-            back = lax.all_to_all(expert_out, group, 0, 0, tiled=True)
-            z0 = dot((slots[b, :, 0][:, None] == slot_ix[None, :]).astype(BF16), back)
-            z1 = dot((slots[b, :, 1][:, None] == slot_ix[None, :]).astype(BF16), back)
+            results.append(dot(mixed, w_down[0], BF16))
+        near_rows, far_rows = [], []
+        for b in range(n_micro):
+            back = lax.all_to_all(results[b], group, 0, 0, tiled=True, axis_index_groups=halves)
+            back = after(back, results[-1] if b == 0 else far_rows[b - 1])
+            z0 = dot(pick_of(b, 0), back)
+            z1 = dot(pick_of(b, 1), back)
+            near_rows.append((z0[:tokens], z1[:tokens]))
+            p0, p1 = z0[tokens:], z1[tokens:]
+            both = near[b, tokens:, 0:1] & near[b, tokens:, 1:2]
+            gates = peer_gates[b]
+            full = pairs[b][tokens:].astype(F32) + (gates[:, 0:1] * p0 + gates[:, 1:2] * p1)
+            far_rows.append(jnp.where(both, full, p0 + p1).astype(BF16))
+        outs = []
+        for b in range(n_micro):
+            far = lax.ppermute(far_rows[b], 'cp', swap)
+            far = after(far, far_rows[-1] if b == 0 else outs[b - 1])
+            n0, n1 = near[b, :tokens, 0:1], near[b, :tokens, 1:2]
             gates = route_gates[b]
-            outs.append((mid.astype(F32) + gates[:, 0:1] * z0 + gates[:, 1:2] * z1).astype(BF16))
+            far_row = far.astype(F32)
+            c0 = jnp.where(n0, near_rows[b][0], far_row)
+            c1 = jnp.where(n1, near_rows[b][1], far_row)
+            mine = (mids[b].astype(F32) + (gates[:, 0:1] * c0 + gates[:, 1:2] * c1)).astype(BF16)
+            outs.append(jnp.where(n0 | n1, mine, far))
         return jnp.stack(outs)
 
     return jax.shard_map(device_step, mesh=mesh, in_specs=(row_spec, row_spec, row_spec, head_spec, head_spec, head_spec, out_spec, expert_spec, expert_spec, expert_spec), out_specs=row_spec, check_vma=False)

time: 804 us -> 772 us (0.960)
  waiting for transfers between devices: 483 us -> 410 us
  starting transfers between devices: 25.8 us -> 42.9 us
  other arithmetic: 3.63 us -> 19.2 us
    ppermute x0 -> x10, waiting for transfers between devices: none -> 262 us  [the longest x2 107 us: device_step(): overs.append(lax.ppermute(sent[b], 'tp', other_chip))]
    all_to_all x4, waiting for transfers between devices: 233 us -> 71.9 us  [the longest x2 71.5 us: device_step(): lax.all_to_all(results[b], group, 0, 0, tiled=True, axis_index_groups=hal...]
    reduce_scatter x2 -> x0, waiting for transfers between devices: 156 us -> none  [device_step(): lax.psum_scatter(dot(o, wo), 'tp', scatter_dimension=0, tiled=True)]
    all_gather x2, waiting for transfers between devices: 70.7 us -> 33.7 us  [device_step(): x_half = lax.all_gather(x_own, 'tp', axis=0, tiled=True)]
    all_gather x2, waiting for transfers between devices: 22.4 us -> 42.4 us  [device_step(): kv_all = lax.all_gather(kv, 'cp', axis=0)]
    ppermute x0 -> x10, starting transfers between devices: none -> 13.9 us  [the longest x2 7.26 us: device_step(): far = lax.ppermute(far_rows[b], 'cp', swap)]
    dot_general x18 -> x20, matrix products: 202 us -> 204 us  [dot(): return jnp.dot(a, b, preferred_element_type=F32).astype(out)]
  transfers between devices with their start and end apart: 10 -> 18, of which waited for: 8 -> 14; matrix products, arithmetic and copies ran while one was open for 26% -> 28% of each run, Pallas kernels for 6% -> 3%
where the time goes in v2:
time: 772 us; the launch traced here: 759 us
  waiting for transfers between devices  410 us (53%)
  matrix products  204 us (26%)
  Pallas kernels  47.8 us (6%)
  starting transfers between devices  42.9 us (6%)
  local copies, waits for them, and re-layouts  20.7 us (3%)
  other arithmetic  19.2 us (2%)
  between operations  14.2 us (2%)
    dot_general x20, matrix products, dot(): return jnp.dot(a, b, preferred_element_type=F32).astype(out)  204 us
    ppermute x2, waiting for transfers between devices, device_step(): overs.append(lax.ppermute(sent[b], 'tp', other_chip))  107 us
    ppermute x2, waiting for transfers between devices, device_step(): peers.append(lax.ppermute(mids[b], 'cp', swap))  90.6 us
    all_to_all x2, waiting for transfers between devices, device_step(): lax.all_to_all(results[b], group, 0, 0, tiled=True, axis_index_groups=hal...  71.5 us
    ppermute x2, waiting for transfers between devices, device_step(): far = lax.ppermute(far_rows[b], 'cp', swap)  56.5 us
    pallas_call x2, Pallas kernels, attend(): pl.pallas_call(lambda *refs: attend_kernel(cp_size, heads, *refs), out_sh...  47.8 us
    all_gather x2, waiting for transfers between devices, device_step(): kv_all = lax.all_gather(kv, 'cp', axis=0)  42.4 us
    all_gather x2, waiting for transfers between devices, device_step(): x_half = lax.all_gather(x_own, 'tp', axis=0, tiled=True)  33.7 us
  transfers between devices with their start and end apart: 18, of which 14 were waited for; matrix products, arithmetic and copies ran while one was open for 28% of the time, Pallas kernels for 3%

profile of v2, /device:TPU:13, one launch (start us, length us, event | category | flops | bytes accessed | tf_op | source)
XLA Modules:
  0.0 759.3 jit_solution(7349841357934047321)
XLA Ops:
  19.1 33.7 %all-gather.10.cloned.1.call-done = bf16[1,768,3584]{2,1,0:T(8,128)(2,1)} async-done(((bf16[1,192,3584]{2,1,0:T(8,128)(2,1)}), bf16[1,768,3584]{2,1,0:T(8,128)(2,1)}) %all-gather.10.cloned.1.call-update) | async-done | bytes 5505040 | tf_op jit(solution)/shard_map/all_gather | solution.py:130
  52.8 5.1 convolution_convert_fusion.5
  58.0 9.6 %copy.26 = bf16[3584,7,128]{0,2,1:T(8,128)(2,1)} copy(bf16[3584,7,128]{2,0,1:T(8,128)(2,1)} %param.13) | data formatting | bytes 12845056 | tf_op args[3]
  67.7 9.8 %convolution_convert_fusion.3.refs_1_ = bf16[768,896]{1,0:T(8,128)(2,1)S(1)} fusion(bf16[768,3584]{1,0:T(8,128)(2,1)} %bitcast.135, bf16[3584,896]{0,1:T(8,128)(2,1)} %bitcast.113), kind=kOutput, calls=%fused_computation.57 | convolution fusion | flops 4933189632 | bytes 13303808 | tf_op jit(solution)/shard_map/dot_general | solution.py:78
  77.5 16.8 %all-gather.12.cloned.1.call-done = bf16[3072,256]{1,0:T(8,128)(2,1)} async-done(((bf16[768,256]{1,0:T(8,128)(2,1)}), bf16[3072,256]{1,0:T(8,128)(2,1)}) %all-gather.12.cloned.1.call-update) | async-done | bytes 1572880 | tf_op jit(solution)/shard_map/all_gather | solution.py:136
  95.7 23.9 %shard_map.100 = bf16[768,896]{1,0:T(8,128)(2,1)S(1)} custom-call(s32[1]{0:T(128)} %bitcast.1.refs_0_, bf16[768,896]{1,0:T(8,128)(2,1)S(1)} %convolution_convert_fusion.3.refs_1_, bf16[4,768,256]{2,1,0:T(8,128)(2,1)S(1)} %bitcast.107), custom_call_target="tpu_custom_call" | custom-call | flops 7134511104 | bytes 4325376 | tf_op jit(solution)/shard_map/pallas_call | solution.py:66
  119.7 7.8 %fusion.61 = f32[384,3584]{1,0:T(8,128)} fusion(bf16[896,3584]{1,0:T(8,128)(2,1)} %bitcast.130, bf16[192,896]{1,0:T(8,128)(2,1)S(1)} %get-tuple-element.60, bf16[192,896]{1,0:T(8,128)(2,1)S(1)} %get-tuple-element.59), kind=kOutput, calls=%fused_computation.76 | convolution fusion | flops 2467627008 | bytes 12615680 | tf_op jit(solution)/shard_map/dot_general | solution.py:78
  128.8 5.1 fusion.65
  141.9 4.9 convolution_convert_fusion.4
  146.9 9.8 %convolution_convert_fusion.2.refs_1_ = bf16[768,896]{1,0:T(8,128)(2,1)S(1)} fusion(bf16[768,3584]{1,0:T(8,128)(2,1)} %all-gather.8.cloned.1.call-done, bf16[3584,896]{0,1:T(8,128)(2,1)} %bitcast.114), kind=kOutput, calls=%fused_computation.56 | convolution fusion | flops 4933189632 | bytes 13303808 | tf_op jit(solution)/shard_map/dot_general | solution.py:78
  156.6 25.6 %all-gather.14.cloned.1.call-done = bf16[3072,256]{1,0:T(8,128)(2,1)} async-done(((bf16[768,256]{1,0:T(8,128)(2,1)}), bf16[3072,256]{1,0:T(8,128)(2,1)}) %all-gather.14.cloned.1.call-update) | async-done | bytes 1572880 | tf_op jit(solution)/shard_map/all_gather | solution.py:136
  183.6 23.9 %shard_map.101 = bf16[768,896]{1,0:T(8,128)(2,1)S(1)} custom-call(s32[1]{0:T(128)} %bitcast.1.refs_0_, bf16[768,896]{1,0:T(8,128)(2,1)S(1)} %convolution_convert_fusion.2.refs_1_, bf16[4,768,256]{2,1,0:T(8,128)(2,1)S(1)} %bitcast.108), custom_call_target="tpu_custom_call" | custom-call | flops 7134511104 | bytes 4325376 | tf_op jit(solution)/shard_map/pallas_call | solution.py:66
  207.6 5.3 fusion.69
  214.6 5.3 fusion.73
  223.5 51.9 %collective-permute-done.3 = f32[192,3584]{1,0:T(8,128)S(1)} collective-permute-done((f32[192,3584]{1,0:T(8,128)S(1)}, f32[192,3584]{1,0:T(8,128)S(1)}, u32[]{:S(2)}, u32[]{:S(2)}) %collective-permute-start.3) | collective-permute-done | bytes 2752544 | tf_op jit(solution)/shard_map/ppermute | solution.py:142
  279.6 54.8 %collective-permute-done.6 = f32[192,3584]{1,0:T(8,128)S(1)} collective-permute-done((f32[192,3584]{1,0:T(8,128)S(1)}, f32[192,3584]{1,0:T(8,128)S(1)}, u32[]{:S(2)}, u32[]{:S(2)}) %collective-permute-start.6) | collective-permute-done | bytes 2752544 | tf_op jit(solution)/shard_map/ppermute | solution.py:142
  342.5 9.6 %all-to-all-start = ((bf16[8,96,3584]{2,1,0:T(8,128)(2,1)}), bf16[8,96,3584]{2,1,0:T(8,128)(2,1)}, u32[]{:S(2)}, u32[]{:S(2)}) async-start(bf16[8,96,3584]{2,1,0:T(8,128)(2,1)} %bitcast.120), calls=%async_computation | async-start | bytes 11010048 | tf_op jit(solution)/shard_map/all_to_all | solution.py:162
  352.2 88.2 %collective-permute-done.7 = bf16[192,3584]{1,0:T(8,128)(2,1)S(1)} collective-permute-done((bf16[192,3584]{1,0:T(8,128)(2,1)S(1)}, bf16[192,3584]{1,0:T(8,128)(2,1)S(1)}, u32[]{:S(2)}, u32[]{:S(2)}) %collective-permute-start.7) | collective-permute-done | bytes 1376288 | tf_op jit(solution)/shard_map/ppermute | solution.py:149
  446.4 5.8 all-to-all-start.2
  452.2 19.8 %fusion.10 = f32[768,2560]{1,0:T(8,128)S(1)} fusion(bf16[768,3584]{1,0:T(8,128)(2,1)} %bitcast.16, bf16[1,3584,2560]{2,1,0:T(8,128)(2,1)} %param.17), kind=kOutput, calls=%fused_computation.10 | convolution fusion | flops 14092861440 | bytes 31719424 | tf_op jit(solution)/shard_map/dot_general | solution.py:78
  472.0 20.1 %multiply_convert_fusion.1.clone.4 = bf16[768,2560]{1,0:T(8,128)(2,1)S(1)} fusion(f32[768,2560]{1,0:T(8,128)S(1)} %fusion.10, bf16[768,3584]{1,0:T(8,128)(2,1)} %bitcast.16, bf16[1,3584,2560]{2,1,0:T(8,128)(2,1)} %param.18), kind=kOutput, calls=%fused_computation.13.clone.clone.clone.1 | convolution fusion | flops 14104657920 | bytes 35651584 | tf_op jit(solution)/shard_map/dot_general | solution.py:78
  492.1 19.9 %fusion.12 = bf16[768,3584]{1,0:T(8,128)(2,1)} fusion(bf16[1,2560,3584]{2,1,0:T(8,128)(2,1)} %param.19, bf16[768,2560]{1,0:T(8,128)(2,1)S(1)} %multiply_convert_fusion.1.clone.4), kind=kOutput, calls=%fused_computation.16 | convolution fusion | flops 14095613952 | bytes 27787264 | tf_op jit(solution)/shard_map/dot_general | solution.py:78
  512.5 6.6 all-to-all-start.1
  519.1 19.7 %fusion.8 = f32[768,2560]{1,0:T(8,128)S(1)} fusion(bf16[768,3584]{1,0:T(8,128)(2,1)} %bitcast.23, bf16[1,3584,2560]{2,1,0:T(8,128)(2,1)} %param.17), kind=kOutput, calls=%fused_computation.8 | convolution fusion | flops 14092861440 | bytes 31719424 | tf_op jit(solution)/shard_map/dot_general | solution.py:78
  538.8 20.1 %multiply_convert_fusion.clone.2 = bf16[768,2560]{1,0:T(8,128)(2,1)S(1)} fusion(f32[768,2560]{1,0:T(8,128)S(1)} %fusion.8, bf16[768,3584]{1,0:T(8,128)(2,1)} %bitcast.23, bf16[1,3584,2560]{2,1,0:T(8,128)(2,1)} %param.18), kind=kOutput, calls=%fused_computation.12.clone.clone.clone | convolution fusion | flops 14104657920 | bytes 35651584 | tf_op jit(solution)/shard_map/dot_general | solution.py:78
  558.9 19.9 %fusion.15 = bf16[768,3584]{1,0:T(8,128)(2,1)} fusion(bf16[1,2560,3584]{2,1,0:T(8,128)(2,1)} %param.19, bf16[768,2560]{1,0:T(8,128)(2,1)S(1)} %multiply_convert_fusion.clone.2), kind=kOutput, calls=%fused_computation.17 | convolution fusion | flops 14095613952 | bytes 27787264 | tf_op jit(solution)/shard_map/dot_general | solution.py:78
  579.4 6.8 all-to-all-start.3
  591.6 6.9 fusion.58
  604.0 71.0 %all-to-all-done.3 = bf16[8,96,3584]{2,1,0:T(8,128)(2,1)} async-done(((bf16[8,96,3584]{2,1,0:T(8,128)(2,1)}), bf16[8,96,3584]{2,1,0:T(8,128)(2,1)}, u32[]{:S(2)}, u32[]{:S(2)}) %all-to-all-start.3) | async-done | bytes 5505056 | tf_op jit(solution)/shard_map/all_to_all | solution.py:170
  674.9 5.1 fusion.59
  680.1 5.1 fusion.60
  692.3 56.5 %collective-permute-done.9 = bf16[192,3584]{1,0:T(8,128)(2,1)S(1)} collective-permute-done((bf16[192,3584]{1,0:T(8,128)(2,1)S(1)}, bf16[192,3584]{1,0:T(8,128)(2,1)S(1)}, u32[]{:S(2)}, u32[]{:S(2)}) %collective-permute-start.9) | collective-permute-done | bytes 1376288 | tf_op jit(solution)/shard_map/ppermute | solution.py:182
  (151 shorter events, 70.6 us)
Async XLA Ops:
  6.5 46.3 %all-gather.10.cloned.1.call-start = ((), (), s32[]{:S(2)}) async-start(), calls=%async_computation.5 | async-start | bytes 6881280 | tf_op jit(solution)/shard_map/all_gather | solution.py:130
  10.1 42.7 %copy-start.30 = (bf16[3584,1,128]{2,0,1:T(8,128)(2,1)S(1)}, bf16[3584,1,128]{2,0,1:T(8,128)(2,1)}, u32[]{:S(2)}) copy-start(bf16[3584,1,128]{2,0,1:T(8,128)(2,1)} %param.15) | copy-start | bytes 2752516
  10.1 84.1 %all-gather.12.cloned.1.call-start = ((), (), s32[]{:S(2)}) async-start(), calls=%async_computation.6 | async-start | bytes 1966080 | tf_op jit(solution)/shard_map/all_gather | solution.py:136
  10.2 3.4 collective-permute-start
  12.6 6.5 collective-permute-start.1
  19.0 39.0 %copy-start.11 = (pred[2,384,2]{2,1,0:T(8,128)(4,1)}, pred[2,384,2]{2,1,0:T(8,128)(4,1)S(1)}, u32[]{:S(2)}) copy-start(pred[2,384,2]{2,1,0:T(8,128)(4,1)S(1)} %gt.13) | copy-start | bytes 4612
  19.1 38.9 %copy-start.28 = (f32[2,192,2]{1,2,0:T(2,128)}, f32[2,192,2]{1,2,0:T(2,128)S(1)}, u32[]{:S(2)}) copy-start(f32[2,192,2]{1,2,0:T(2,128)S(1)} %collective-permute-done.1) | copy-start | bytes 9220
  58.0 83.9 %all-gather.8.cloned.1.call-start = ((), (), s32[]{:S(2)}) async-start(), calls=%async_computation.4 | async-start | bytes 6881280 | tf_op jit(solution)/shard_map/all_gather | solution.py:130
  67.6 114.5 %all-gather.14.cloned.1.call-start = ((), (), s32[]{:S(2)}) async-start(), calls=%async_computation.7 | async-start | bytes 1966080 | tf_op jit(solution)/shard_map/all_gather | solution.py:136
  127.5 10.8 %collective-permute-start.2 = (f32[384,3584]{1,0:T(8,128)}, f32[384,3584]{1,0:T(8,128)}, u32[]{:S(2)}, u32[]{:S(2)}) collective-permute-start(f32[384,3584]{1,0:T(8,128)} %fusion.61), channel_id=1, source_target_pairs={{0,1},{1,0},{2,3},{3,2},{4,5},{5,4},{6,7},{7,6},{8,9},{9,8},{10,11... | collective-permute-start | bytes 16515080 | tf_op jit(solution)/shard_map/ppermute | solution.py:139
  213.0 9.9 %collective-permute-start.4 = (f32[384,3584]{1,0:T(8,128)S(1)}, f32[384,3584]{1,0:T(8,128)S(1)}, u32[]{:S(2)}, u32[]{:S(2)}) collective-permute-start(f32[384,3584]{1,0:T(8,128)S(1)} %fusion.69), channel_id=1, source_target_pairs={{0,1},{1,0},{2,3},{3,2},{4,5},{5,4},{6,7},{7,6},{8,9},{9,8},{10,11... | collective-permute-start | bytes 16515080 | tf_op jit(solution)/shard_map/ppermute | solution.py:139
  214.2 61.1 %collective-permute-start.3 = (f32[192,3584]{1,0:T(8,128)S(1)}, f32[192,3584]{1,0:T(8,128)S(1)}, u32[]{:S(2)}, u32[]{:S(2)}) collective-permute-start(f32[192,3584]{1,0:T(8,128)S(1)} %copy-done.10), channel_id=1, source_target_pairs={{0,2},{1,3},{2,0},{3,1},{4,6},{5,7},{6,4},{7,5},{8,10},{9,11},{10,... | collective-permute-start | bytes 8257544 | tf_op jit(solution)/shard_map/ppermute | solution.py:142
  214.5 60.9 %slice-start.4 = ((s8[5505024]{0:T(1024)(128)(4,1)}), s8[4194304]{0:T(1024)(128)(4,1)S(1)}, s32[]{:S(2)}) async-start(s8[5505024]{0:T(1024)(128)(4,1)} %bitcast.115), calls=%async_computation.12 | async-start | bytes 8388608
  214.5 60.8 %slice-start.5 = ((s8[5505024]{0:T(1024)(128)(4,1)}), s8[1310720]{0:T(1024)(128)(4,1)S(1)}, s32[]{:S(2)}) async-start(s8[5505024]{0:T(1024)(128)(4,1)} %bitcast.115), calls=%async_computation.13 | async-start | bytes 2621440
  219.9 55.5 %copy-start.4 = (bf16[2,192,3584]{2,1,0:T(8,128)(2,1)S(1)}, bf16[2,192,3584]{2,1,0:T(8,128)(2,1)}, u32[]{:S(2)}) copy-start(bf16[2,192,3584]{2,1,0:T(8,128)(2,1)} %param.10) | copy-start | bytes 8257540
  223.2 111.2 %collective-permute-start.6 = (f32[192,3584]{1,0:T(8,128)S(1)}, f32[192,3584]{1,0:T(8,128)S(1)}, u32[]{:S(2)}, u32[]{:S(2)}) collective-permute-start(f32[192,3584]{1,0:T(8,128)S(1)} %slice_add_fusion.1), channel_id=1, source_target_pairs={{0,2},{1,3},{2,0},{3,1},{4,6},{5,7},{6,4},{7,5},{8,10},{9,11},{10,... | collective-permute-start | bytes 8257544 | tf_op jit(solution)/shard_map/ppermute | solution.py:142
  278.1 59.6 %copy-start.6 = (bf16[192,3584]{1,0:T(8,128)(2,1)}, bf16[192,3584]{1,0:T(8,128)(2,1)S(1)}, u32[]{:S(2)}) copy-start(bf16[192,3584]{1,0:T(8,128)(2,1)S(1)} %fusion.43) | copy-start | bytes 4128772
  278.1 59.5 %collective-permute-start.5 = (bf16[192,3584]{1,0:T(8,128)(2,1)S(1)}, bf16[192,3584]{1,0:T(8,128)(2,1)S(1)}, u32[]{:S(2)}, u32[]{:S(2)}) collective-permute-start(bf16[192,3584]{1,0:T(8,128)(2,1)S(1)} %fusion.43), channel_id=1, source_target_pairs={{0,8},{4,12},{8,0},{12,4},{1,9},{5,13},{9,1},{13,5},{2,10},{6,14},... | collective-permute-start | bytes 4128776 | tf_op jit(solution)/shard_map/ppermute | solution.py:149
  279.5 58.1 %copy-start.21 = (s32[384]{0:T(512)}, s32[384]{0:T(512)S(1)}, u32[]{:S(2)}) copy-start(s32[384]{0:T(512)S(1)} %get-tuple-element.41) | copy-start | bytes 4612
  279.5 58.1 %copy-start.23 = (s32[384]{0:T(512)}, s32[384]{0:T(512)S(1)}, u32[]{:S(2)}) copy-start(s32[384]{0:T(512)S(1)} %get-tuple-element.42) | copy-start | bytes 4612
  279.6 160.9 %copy-start.17 = (s32[384]{0:T(512)}, s32[384]{0:T(512)S(1)}, u32[]{:S(2)}) copy-start(s32[384]{0:T(512)S(1)} %get-tuple-element.40) | copy-start | bytes 4612
  279.6 160.9 %copy-start.19 = (s32[384]{0:T(512)}, s32[384]{0:T(512)S(1)}, u32[]{:S(2)}) copy-start(s32[384]{0:T(512)S(1)} %get-tuple-element.39) | copy-start | bytes 4612
  335.3 105.2 %copy-start.8 = (bf16[192,3584]{1,0:T(8,128)(2,1)}, bf16[192,3584]{1,0:T(8,128)(2,1)S(1)}, u32[]{:S(2)}) copy-start(bf16[192,3584]{1,0:T(8,128)(2,1)S(1)} %fusion.40) | copy-start | bytes 4128772
  342.5 103.8 %all-to-all-start = ((bf16[8,96,3584]{2,1,0:T(8,128)(2,1)}), bf16[8,96,3584]{2,1,0:T(8,128)(2,1)}, u32[]{:S(2)}, u32[]{:S(2)}) async-start(bf16[8,96,3584]{2,1,0:T(8,128)(2,1)} %bitcast.120), calls=%async_computation | async-start | bytes 11010048 | tf_op jit(solution)/shard_map/all_to_all | solution.py:162
  352.2 88.3 %collective-permute-start.7 = (bf16[192,3584]{1,0:T(8,128)(2,1)S(1)}, bf16[192,3584]{1,0:T(8,128)(2,1)S(1)}, u32[]{:S(2)}, u32[]{:S(2)}) collective-permute-start(bf16[192,3584]{1,0:T(8,128)(2,1)S(1)} %fusion.40), channel_id=1, source_target_pairs={{0,8},{4,12},{8,0},{12,4},{1,9},{5,13},{9,1},{13,5},{2,10},{6,14},... | collective-permute-start | bytes 4128776 | tf_op jit(solution)/shard_map/ppermute | solution.py:149
  446.4 66.1 %all-to-all-start.2 = ((bf16[8,96,3584]{2,1,0:T(8,128)(2,1)}), bf16[8,96,3584]{2,1,0:T(8,128)(2,1)}, u32[]{:S(2)}, u32[]{:S(2)}) async-start(bf16[8,96,3584]{2,1,0:T(8,128)(2,1)} %bitcast.119), calls=%async_computation.2 | async-start | bytes 11010048 | tf_op jit(solution)/shard_map/all_to_all | solution.py:162
  512.5 66.9 %all-to-all-start.1 = ((bf16[8,96,3584]{2,1,0:T(8,128)(2,1)}), bf16[8,96,3584]{2,1,0:T(8,128)(2,1)}, u32[]{:S(2)}, u32[]{:S(2)}) async-start(bf16[8,96,3584]{2,1,0:T(8,128)(2,1)} %bitcast.118), calls=%async_computation.1 | async-start | bytes 11010048 | tf_op jit(solution)/shard_map/all_to_all | solution.py:170
  579.4 95.6 %all-to-all-start.3 = ((bf16[8,96,3584]{2,1,0:T(8,128)(2,1)}), bf16[8,96,3584]{2,1,0:T(8,128)(2,1)}, u32[]{:S(2)}, u32[]{:S(2)}) async-start(bf16[8,96,3584]{2,1,0:T(8,128)(2,1)} %bitcast.117), calls=%async_computation.3 | async-start | bytes 11010048 | tf_op jit(solution)/shard_map/all_to_all | solution.py:170
  598.5 76.4 %copy-start.20 = (s32[384]{0:T(512)S(1)}, s32[384]{0:T(512)}, u32[]{:S(2)}) copy-start(s32[384]{0:T(512)} %copy-done.19) | copy-start | bytes 4612
  600.9 89.6 %collective-permute-start.8 = (bf16[192,3584]{1,0:T(8,128)(2,1)S(1)}, bf16[192,3584]{1,0:T(8,128)(2,1)S(1)}, u32[]{:S(2)}, u32[]{:S(2)}) collective-permute-start(bf16[192,3584]{1,0:T(8,128)(2,1)S(1)} %select_convert_fusion.1), channel_id=1, source_target_pairs={{0,8},{4,12},{8,0},{12,4},{1,9},{5,13},{9,1},{13,5},{2,10},{6,14},... | collective-permute-start | bytes 4128776 | tf_op jit(solution)/shard_map/ppermute | solution.py:182
  686.3 62.5 %collective-permute-start.9 = (bf16[192,3584]{1,0:T(8,128)(2,1)S(1)}, bf16[192,3584]{1,0:T(8,128)(2,1)S(1)}, u32[]{:S(2)}, u32[]{:S(2)}) collective-permute-start(bf16[192,3584]{1,0:T(8,128)(2,1)S(1)} %select_convert_fusion), channel_id=1, source_target_pairs={{0,8},{4,12},{8,0},{12,4},{1,9},{5,13},{9,1},{13,5},{2,10},{6,14},... | collective-permute-start | bytes 4128776 | tf_op jit(solution)/shard_map/ppermute | solution.py:182
  690.5 58.3 %copy-start.9 = (bf16[192,3584]{1,0:T(8,128)(2,1)S(1)}, bf16[192,3584]{1,0:T(8,128)(2,1)}, u32[]{:S(2)}) copy-start(bf16[192,3584]{1,0:T(8,128)(2,1)} %copy-done.8) | copy-start | bytes 4128772
  (25 other events, 162.2 us)
Sparse Core Ops, SparseCore 0:
  10.3 42.5 all-gather.9
  58.1 36.1 all-gather.11
  95.8 41.8 all-gather.7
  147.0 35.1 all-gather.13
